TPU v7x, 32 devices: a whole 2x2x4 slice. The times are simulated.
32 devices in a mesh: row: 8 (over z, y), col: 4 (over x, core).
Axes of the slice: x: 2, y: 2, z: 4, core: 2. Of those that a mesh axis runs over, the one named last changes fastest.
Arguments:
- matrix_tiles: bfloat16 [8, 4, 96, 256, 256], P('row', 'col'), may hold values from -0.078125 to 0.078125
- tile_rows: int32 [8, 4, 96], P('row', 'col'), may hold values from 0 to 7, as said below
- tile_cols: int32 [8, 4, 96], P('row', 'col'), may hold values from 0 to 15
- tile_count: int32 [8, 4], P('row', 'col'), may hold values from 24 to 96, as said below
- x_start: float32 [16384, 256], P(('col', 'row')), may hold values from -5 to 5
- y_start: float32 [16384, 256], P(('row', 'col')), may hold values from 0 to 1
- cost_vector: float32 [16384, 256], P(('col', 'row')), may hold values from -6 to 6
- right_side: float32 [16384, 256], P(('row', 'col')), may hold values from -6 to 6
- lower_bound: float32 [16384, 256], P(('col', 'row')), may hold values from -1.5 to -0.3
- upper_bound: float32 [16384, 256], P(('col', 'row')), may hold values from 0.3 to 1.5
- step_primal: float32 [256], replicated, may hold values from 0.2 to 0.45
- step_dual: float32 [256], replicated, may hold values from 0.2 to 0.45
Outputs:
- primal_out: float32 [16384, 256], P(('col', 'row'))
- dual_out: float32 [16384, 256], P(('row', 'col'))
Inputs may be any that keep to these rules, and one draw needn't show every extreme that they name: Within one grid cell the pairs (tile_rows, tile_cols) of its slots are all different. `tile_count`: some grid cell has 96 used slots in every draw; slots at or above a cell's count are not part of A.
All inputs are finite; a program needn't handle non-finite values.
Results may differ from a plain program's by a relative error of at most 0.001.
Values may be sent and summed in bfloat16 or wider, within the bound.
A program may use at most 128 MiB of HBM per device.

v0:
```python
import jax
import jax.numpy as jnp
from jax import lax
from jax.sharding import PartitionSpec as P

NR_DEV = 8
SLOT_BLOCK = 16
eps = 1e-06


def forward_part(my_tiles, my_rows, my_cols, slot_count, segment):
    edge = my_tiles.shape[-1]
    batch_width = segment.shape[-1]
    x_tiles = segment.reshape(-1, edge, batch_width)
    slot_ids = jnp.arange(SLOT_BLOCK, dtype=jnp.int32)

    def forward_block_step(block_index, running):
        first_slot = block_index * SLOT_BLOCK
        tile_block = lax.dynamic_slice_in_dim(my_tiles, first_slot, SLOT_BLOCK, 0)
        row_block = lax.dynamic_slice_in_dim(my_rows, first_slot, SLOT_BLOCK, 0)
        col_block = lax.dynamic_slice_in_dim(my_cols, first_slot, SLOT_BLOCK, 0)
        in_use = first_slot + slot_ids < slot_count
        pieces = jnp.take(x_tiles, col_block, axis=0)
        products = jnp.einsum(
            "sij,sjb->sib", tile_block, pieces, preferred_element_type=jnp.float32
        )
        products = jnp.where(in_use[:, None, None], products, jnp.zeros_like(products))
        return running.at[row_block].add(products)

    blocks = (slot_count + SLOT_BLOCK - 1) // SLOT_BLOCK
    begin = jnp.zeros((NR_DEV, edge, batch_width), jnp.float32)
    return lax.fori_loop(0, blocks, forward_block_step, begin).reshape(-1, batch_width)


def backward_part(my_tiles, my_rows, my_cols, slot_count, segment, col_tiles):
    edge = my_tiles.shape[-1]
    batch_width = segment.shape[-1]
    y_tiles = segment.reshape(-1, edge, batch_width)
    slot_ids = jnp.arange(SLOT_BLOCK, dtype=jnp.int32)

    def backward_block_step(block_index, running):
        first_slot = block_index * SLOT_BLOCK
        tile_block = lax.dynamic_slice_in_dim(my_tiles, first_slot, SLOT_BLOCK, 0)
        row_block = lax.dynamic_slice_in_dim(my_rows, first_slot, SLOT_BLOCK, 0)
        col_block = lax.dynamic_slice_in_dim(my_cols, first_slot, SLOT_BLOCK, 0)
        in_use = first_slot + slot_ids < slot_count
        pieces = jnp.take(y_tiles, row_block, axis=0)
        products = jnp.einsum(
            "sij,sib->sjb", tile_block, pieces, preferred_element_type=jnp.float32
        )
        products = jnp.where(in_use[:, None, None], products, jnp.zeros_like(products))
        return running.at[col_block].add(products)

    blocks = (slot_count + SLOT_BLOCK - 1) // SLOT_BLOCK
    begin = jnp.zeros((col_tiles, edge, batch_width), jnp.float32)
    return lax.fori_loop(0, blocks, backward_block_step, begin).reshape(-1, batch_width)


def body(
    matrix_tiles,
    tile_rows,
    tile_cols,
    tile_count,
    x_start,
    y_start,
    cost_vector,
    right_side,
    lower_bound,
    upper_bound,
    step_primal,
    step_dual,
):
    my_tiles = matrix_tiles[0, 0]
    my_rows = tile_rows[0, 0]
    my_cols = tile_cols[0, 0]
    slot_count = tile_count[0, 0]
    row_devices = lax.axis_size("row")
    col_devices = lax.axis_size("col")
    share = x_start.shape[0]
    edge = my_tiles.shape[-1]
    col_tiles = share * row_devices // edge
    total_cols = share * row_devices * col_devices
    total_rows = y_start.shape[0] * row_devices * col_devices

    def dual_rows(values):
        return lax.all_gather(values.astype(jnp.bfloat16), "col", axis=0, tiled=True)

    def row_sums(segment):
        return lax.psum_scatter(
            forward_part(my_tiles, my_rows, my_cols, slot_count, segment),
            "col",
            scatter_dimension=0,
            tiled=True,
        )

    x_base, cost_seg, lower_seg, upper_seg = (x_start, cost_vector, lower_bound, upper_bound)

    def column_sums(segment):
        partial_value = backward_part(my_tiles, my_rows, my_cols, slot_count, segment, col_tiles)
        return lax.psum_scatter(partial_value, "row", scatter_dimension=0, tiled=True)

    def spread(ahead):
        return lax.all_gather(ahead, "row", axis=0, tiled=True)

    grad_zero = column_sums(dual_rows(y_start))
    primal_one = jnp.clip(x_base - step_primal * (cost_seg - grad_zero), lower_seg, upper_seg)
    primal_diff = primal_one - x_base
    move_primal = jnp.sum(primal_diff * primal_diff, axis=0)
    image_one = row_sums(spread((2.0 * primal_one - x_base).astype(jnp.bfloat16)))
    dual_one = jnp.maximum(y_start + step_dual * (right_side - image_one), 0.0)
    dual_diff = dual_one - y_start
    move_dual = jnp.sum(dual_diff * dual_diff, axis=0)
    move_primal, move_dual = lax.psum((move_primal, move_dual), ("row", "col"))
    weight = jnp.sqrt((move_dual / total_rows + eps) / (move_primal / total_cols + eps))
    grad_one = column_sums(dual_rows(dual_one))
    primal_two = jnp.clip(
        primal_one - step_primal / weight * (cost_seg - grad_one), lower_seg, upper_seg
    )
    image_two = row_sums(spread((2.0 * primal_two - primal_one).astype(jnp.bfloat16)))
    dual_out = jnp.maximum(dual_one + step_dual * weight * (right_side - image_two), 0.0)
    return (primal_two, dual_out)


def solution(mesh):
    placed = (
        P("row", "col", None, None, None),
        P("row", "col", None),
        P("row", "col", None),
        P("row", "col"),
        P(("col", "row"), None),
        P(("row", "col"), None),
        P(("col", "row"), None),
        P(("row", "col"), None),
        P(("col", "row"), None),
        P(("col", "row"), None),
        P(),
        P(),
    )
    return jax.shard_map(
        body,
        mesh=mesh,
        in_specs=placed,
        out_specs=(P(("col", "row"), None), P(("row", "col"), None)),
        check_vma=False,
    )
```

profile of v0, /device:TPU:0, one launch (start us, length us, event | category | flops | bytes accessed | tf_op | source)
XLA Modules:
  0.0 772.5 jit_solution(1718431034138353426)
XLA Ops:
  9.7 16.6 %copy.14 = bf16[96,256,256]{1,2,0:T(8,128)(2,1)} copy(bf16[96,256,256]{2,1,0:T(8,128)(2,1)} %bitcast.19) | data formatting | bytes 25165824
  31.9 91.8 %while.44 = (s32[]{:T(128)}, f32[16,256,256]{2,1,0:T(8,128)}, s32[]{:T(128)}, s32[96]{0:T(128)S(1)}, s32[]{:T(128)}, /*index=5*/bf16[96,256,256]{1,2,0:T(8,128)(...) while((s32[]{:T(128)}, f32[16,256,256]{2,1,0:T(8,128)}, ...), condition=%wide.region_2.4_spmd.clone, body=%wide.region_0.3_spmd.clone.sunk | while | flops 540017856 | bytes 25170616 | solution.py:56
  33.4 4.3 convolution_select_fusion.8
  37.8 9.5 %scatter_fusion = f32[16,256,256]{2,1,0:T(8,128)} fusion(f32[16,256,256]{2,1,0:T(8,128)} %get-tuple-element.615, s32[16]{0:T(128)S(1)} %compare_select_fusion.16, f32[16,256,256]{2,1,0:T(8,128)} %convolution_select_fusion.8), kind=kCustom, calls=%fused_computation.4.clone.clone.1 | custom fusion | flops 1048576 | bytes 12582976 | tf_op jit(solution)/shard_map/while/body/scatter-add | solution.py:52
  48.8 4.3 convolution_select_fusion.8
  53.2 9.5 %scatter_fusion = f32[16,256,256]{2,1,0:T(8,128)} fusion(f32[16,256,256]{2,1,0:T(8,128)} %get-tuple-element.615, s32[16]{0:T(128)S(1)} %compare_select_fusion.16, f32[16,256,256]{2,1,0:T(8,128)} %convolution_select_fusion.8), kind=kCustom, calls=%fused_computation.4.clone.clone.1 | custom fusion | flops 1048576 | bytes 12582976 | tf_op jit(solution)/shard_map/while/body/scatter-add | solution.py:52
  64.1 4.3 convolution_select_fusion.8
  68.5 9.5 %scatter_fusion = f32[16,256,256]{2,1,0:T(8,128)} fusion(f32[16,256,256]{2,1,0:T(8,128)} %get-tuple-element.615, s32[16]{0:T(128)S(1)} %compare_select_fusion.16, f32[16,256,256]{2,1,0:T(8,128)} %convolution_select_fusion.8), kind=kCustom, calls=%fused_computation.4.clone.clone.1 | custom fusion | flops 1048576 | bytes 12582976 | tf_op jit(solution)/shard_map/while/body/scatter-add | solution.py:52
  79.4 4.3 convolution_select_fusion.8
  83.8 9.5 %scatter_fusion = f32[16,256,256]{2,1,0:T(8,128)} fusion(f32[16,256,256]{2,1,0:T(8,128)} %get-tuple-element.615, s32[16]{0:T(128)S(1)} %compare_select_fusion.16, f32[16,256,256]{2,1,0:T(8,128)} %convolution_select_fusion.8), kind=kCustom, calls=%fused_computation.4.clone.clone.1 | custom fusion | flops 1048576 | bytes 12582976 | tf_op jit(solution)/shard_map/while/body/scatter-add | solution.py:52
  94.8 4.3 convolution_select_fusion.8
  99.2 9.3 %scatter_fusion = f32[16,256,256]{2,1,0:T(8,128)} fusion(f32[16,256,256]{2,1,0:T(8,128)} %get-tuple-element.615, s32[16]{0:T(128)S(1)} %compare_select_fusion.16, f32[16,256,256]{2,1,0:T(8,128)} %convolution_select_fusion.8), kind=kCustom, calls=%fused_computation.4.clone.clone.1 | custom fusion | flops 1048576 | bytes 12582976 | tf_op jit(solution)/shard_map/while/body/scatter-add | solution.py:52
  109.9 4.3 convolution_select_fusion.8
  114.3 9.5 %scatter_fusion = f32[16,256,256]{2,1,0:T(8,128)} fusion(f32[16,256,256]{2,1,0:T(8,128)} %get-tuple-element.615, s32[16]{0:T(128)S(1)} %compare_select_fusion.16, f32[16,256,256]{2,1,0:T(8,128)} %convolution_select_fusion.8), kind=kCustom, calls=%fused_computation.4.clone.clone.1 | custom fusion | flops 1048576 | bytes 12582976 | tf_op jit(solution)/shard_map/while/body/scatter-add | solution.py:52
  123.8 86.9 %reduce-scatter.5.cloned.1.call-done = f32[512,256]{1,0:T(8,128)} async-done(((f32[4096,256]{1,0:T(8,128)}), f32[512,256]{1,0:T(8,128)}) %reduce-scatter.5.cloned.1.call-update) | async-done | bytes 524304 | tf_op jit(solution)/shard_map/reduce_scatter | solution.py:100
  213.6 48.8 %all-gather.7.cloned.1.call-done = bf16[4096,256]{1,0:T(8,128)(2,1)} async-done(((bf16[512,256]{1,0:T(8,128)(2,1)}), bf16[4096,256]{1,0:T(8,128)(2,1)}) %all-gather.7.cloned.1.call-update) | async-done | bytes 2097168 | tf_op jit(solution)/shard_map/all_gather | solution.py:103
  262.6 93.1 %while.45 = (s32[]{:T(128)}, f32[8,256,256]{2,1,0:T(8,128)S(1)}, s32[]{:T(128)}, s32[96]{0:T(128)S(1)}, s32[]{:T(128)}, /*index=5*/bf16[96,256,256]{2,1,0:T(8,12...) while((s32[]{:T(128)}, f32[8,256,256]{2,1,0:T(8,128)S(1)}, ...), condition=%wide.region_6.9_spmd.clone, body=%wide.region_4.8_spmd.clone.sunk | while | flops 540017856 | bytes 25170616 | solution.py:32
  266.9 5.0 convolution_select_fusion.9
  271.9 6.1 scatter_fusion.1
  282.4 5.0 convolution_select_fusion.9
  287.5 6.2 scatter_fusion.1
  298.0 4.9 convolution_select_fusion.9
  303.0 6.1 scatter_fusion.1
  313.5 4.9 convolution_select_fusion.9
  318.5 6.2 scatter_fusion.1
  329.0 4.9 convolution_select_fusion.9
  334.0 6.1 scatter_fusion.1
  344.5 4.9 convolution_select_fusion.9
  349.5 6.2 scatter_fusion.1
  357.1 28.9 %reduce-scatter.7.cloned.1.call-done = f32[512,256]{1,0:T(8,128)} async-done(((f32[2048,256]{1,0:T(8,128)}), f32[512,256]{1,0:T(8,128)}) %reduce-scatter.7.cloned.1.call-update) | async-done | bytes 524304 | tf_op jit(solution)/shard_map/reduce_scatter | solution.py:89
  388.8 16.8 %all-gather.9.cloned.1.call-done = bf16[2048,256]{1,0:T(8,128)(2,1)} async-done(((bf16[512,256]{1,0:T(8,128)(2,1)}), bf16[2048,256]{1,0:T(8,128)(2,1)}) %all-gather.9.cloned.1.call-update) | async-done | bytes 1048592 | tf_op jit(solution)/shard_map/all_gather | solution.py:86
  408.0 91.8 %while.46 = (s32[]{:T(128)}, f32[16,256,256]{2,1,0:T(8,128)}, s32[]{:T(128)}, s32[96]{0:T(128)S(1)}, s32[]{:T(128)}, /*index=5*/bf16[96,256,256]{1,2,0:T(8,128)(...) while((s32[]{:T(128)}, f32[16,256,256]{2,1,0:T(8,128)}, ...), condition=%wide.region_14.17_spmd.clone, body=%wide.region_12.16_spmd.clone.sunk | while | flops 540017856 | bytes 25170616 | solution.py:56
  409.4 4.3 convolution_select_fusion.10
  413.8 9.5 %scatter_fusion.2 = f32[16,256,256]{2,1,0:T(8,128)} fusion(f32[16,256,256]{2,1,0:T(8,128)} %get-tuple-element.687, s32[16]{0:T(128)S(1)} %compare_select_fusion.18, f32[16,256,256]{2,1,0:T(8,128)} %convolution_select_fusion.10), kind=kCustom, calls=%fused_computation.6.clone.clone.1 | custom fusion | flops 1048576 | bytes 12582976 | tf_op jit(solution)/shard_map/while/body/scatter-add | solution.py:52
  424.8 4.3 convolution_select_fusion.10
  429.2 9.5 %scatter_fusion.2 = f32[16,256,256]{2,1,0:T(8,128)} fusion(f32[16,256,256]{2,1,0:T(8,128)} %get-tuple-element.687, s32[16]{0:T(128)S(1)} %compare_select_fusion.18, f32[16,256,256]{2,1,0:T(8,128)} %convolution_select_fusion.10), kind=kCustom, calls=%fused_computation.6.clone.clone.1 | custom fusion | flops 1048576 | bytes 12582976 | tf_op jit(solution)/shard_map/while/body/scatter-add | solution.py:52
  440.1 4.3 convolution_select_fusion.10
  444.5 9.5 %scatter_fusion.2 = f32[16,256,256]{2,1,0:T(8,128)} fusion(f32[16,256,256]{2,1,0:T(8,128)} %get-tuple-element.687, s32[16]{0:T(128)S(1)} %compare_select_fusion.18, f32[16,256,256]{2,1,0:T(8,128)} %convolution_select_fusion.10), kind=kCustom, calls=%fused_computation.6.clone.clone.1 | custom fusion | flops 1048576 | bytes 12582976 | tf_op jit(solution)/shard_map/while/body/scatter-add | solution.py:52
  455.4 4.3 convolution_select_fusion.10
  459.8 9.5 %scatter_fusion.2 = f32[16,256,256]{2,1,0:T(8,128)} fusion(f32[16,256,256]{2,1,0:T(8,128)} %get-tuple-element.687, s32[16]{0:T(128)S(1)} %compare_select_fusion.18, f32[16,256,256]{2,1,0:T(8,128)} %convolution_select_fusion.10), kind=kCustom, calls=%fused_computation.6.clone.clone.1 | custom fusion | flops 1048576 | bytes 12582976 | tf_op jit(solution)/shard_map/while/body/scatter-add | solution.py:52
  470.7 4.3 convolution_select_fusion.10
  475.1 9.4 %scatter_fusion.2 = f32[16,256,256]{2,1,0:T(8,128)} fusion(f32[16,256,256]{2,1,0:T(8,128)} %get-tuple-element.687, s32[16]{0:T(128)S(1)} %compare_select_fusion.18, f32[16,256,256]{2,1,0:T(8,128)} %convolution_select_fusion.10), kind=kCustom, calls=%fused_computation.6.clone.clone.1 | custom fusion | flops 1048576 | bytes 12582976 | tf_op jit(solution)/shard_map/while/body/scatter-add | solution.py:52
  485.9 4.3 convolution_select_fusion.10
  490.3 9.4 %scatter_fusion.2 = f32[16,256,256]{2,1,0:T(8,128)} fusion(f32[16,256,256]{2,1,0:T(8,128)} %get-tuple-element.687, s32[16]{0:T(128)S(1)} %compare_select_fusion.18, f32[16,256,256]{2,1,0:T(8,128)} %convolution_select_fusion.10), kind=kCustom, calls=%fused_computation.6.clone.clone.1 | custom fusion | flops 1048576 | bytes 12582976 | tf_op jit(solution)/shard_map/while/body/scatter-add | solution.py:52
  499.8 40.9 %all-reduce = (f32[256]{0:T(256)S(1)}, f32[256]{0:T(256)S(1)}) all-reduce(f32[256]{0:T(256)S(1)} %get-tuple-element.372, f32[256]{0:T(256)S(1)} %get-tuple-element.370), channel_id=1, replica_groups=mesh['row'=8,'col'=4] {'row','col'}, use_global_device_ids=true, to_apply=%region_11.14 | all-reduce | flops 512 | bytes 4096 | tf_op jit(solution)/shard_map/psum | solution.py:113
  540.8 47.3 %reduce-scatter.9.cloned.1.call-done = f32[512,256]{1,0:T(8,128)} async-done(((f32[4096,256]{1,0:T(8,128)}), f32[512,256]{1,0:T(8,128)}) %reduce-scatter.9.cloned.1.call-update) | async-done | bytes 524304 | tf_op jit(solution)/shard_map/reduce_scatter | solution.py:100
  590.2 49.3 %all-gather.11.cloned.1.call-done = bf16[4096,256]{1,0:T(8,128)(2,1)} async-done(((bf16[512,256]{1,0:T(8,128)(2,1)}), bf16[4096,256]{1,0:T(8,128)(2,1)}) %all-gather.11.cloned.1.call-update) | async-done | bytes 2097168 | tf_op jit(solution)/shard_map/all_gather | solution.py:103
  639.7 93.7 %while.47 = (s32[]{:T(128)}, f32[8,256,256]{2,1,0:T(8,128)S(1)}, s32[]{:T(128)}, s32[96]{0:T(128)S(1)}, s32[]{:T(128)}, /*index=5*/bf16[96,256,256]{2,1,0:T(8,12...) while((s32[]{:T(128)}, f32[8,256,256]{2,1,0:T(8,128)S(1)}, ...), condition=%wide.region_18.21_spmd.clone, body=%wide.region_16.20_spmd.clone.sunk | while | flops 540017856 | bytes 25170616 | solution.py:32
  640.4 3.7 gather_fusion.3
  644.1 4.9 convolution_select_fusion.11
  649.1 6.1 scatter_fusion.3
  656.0 3.7 gather_fusion.3
  659.7 5.0 convolution_select_fusion.11
  664.7 6.2 scatter_fusion.3
  671.7 3.7 gather_fusion.3
  675.4 4.9 convolution_select_fusion.11
  680.4 6.1 scatter_fusion.3
  691.0 5.0 convolution_select_fusion.11
  696.0 6.2 scatter_fusion.3
  706.6 4.9 convolution_select_fusion.11
  711.6 6.1 scatter_fusion.3
  722.2 5.0 convolution_select_fusion.11
  727.2 6.2 scatter_fusion.3
  734.8 28.9 %reduce-scatter.11.cloned.1.call-done = f32[512,256]{1,0:T(8,128)} async-done(((f32[2048,256]{1,0:T(8,128)}), f32[512,256]{1,0:T(8,128)}) %reduce-scatter.11.cloned.1.call-update) | async-done | bytes 524304 | tf_op jit(solution)/shard_map/reduce_scatter | solution.py:89
  (167 shorter events, 82.7 us)
Async XLA Ops:
  7.2 22.4 %all-gather.5.cloned.1.call-start = ((), (), s32[]{:S(2)}) async-start(), calls=%async_computation.4 | async-start | bytes 1310720 | tf_op jit(solution)/shard_map/all_gather | solution.py:86
  9.0 201.7 %reduce-scatter.5.cloned.1.call-start = ((), (), s32[]{:S(2)}) async-start(), calls=%async_computation.5 | async-start | bytes 4718592 | tf_op jit(solution)/shard_map/reduce_scatter | solution.py:100
  29.6 2.4 copy-start.2
  29.6 2.4 copy-start.18
  29.6 2.4 copy-start.19
  123.7 87.0 %copy-start.9 = (f32[512,256]{1,0:T(8,128)S(1)}, f32[512,256]{1,0:T(8,128)}, u32[]{:S(2)}) copy-start(f32[512,256]{1,0:T(8,128)} %param.33) | copy-start | bytes 1572868
  123.7 87.0 %copy-start.11 = (f32[512,256]{1,0:T(8,128)S(1)}, f32[512,256]{1,0:T(8,128)}, u32[]{:S(2)}) copy-start(f32[512,256]{1,0:T(8,128)} %param.32) | copy-start | bytes 1572868
  123.7 87.0 %copy-start.13 = (f32[512,256]{1,0:T(8,128)S(1)}, f32[512,256]{1,0:T(8,128)}, u32[]{:S(2)}) copy-start(f32[512,256]{1,0:T(8,128)} %param.30) | copy-start | bytes 1572868
  123.7 87.0 %copy-start.17 = (f32[512,256]{1,0:T(8,128)S(1)}, f32[512,256]{1,0:T(8,128)}, u32[]{:S(2)}) copy-start(f32[512,256]{1,0:T(8,128)} %param.28) | copy-start | bytes 1572868
  123.8 87.0 %copy-start.21 = (f32[256]{0:T(256)S(1)}, f32[256]{0:T(256)}, u32[]{:S(2)}) copy-start(f32[256]{0:T(256)} %param.34) | copy-start | bytes 3076
  123.8 138.6 %all-gather.7.cloned.1.call-start = ((), (), s32[]{:S(2)}) async-start(), calls=%async_computation.6 | async-start | bytes 2359296 | tf_op jit(solution)/shard_map/all_gather | solution.py:103
  211.9 0.8 copy-start.6
  213.5 172.5 %reduce-scatter.7.cloned.1.call-start = ((), (), s32[]{:S(2)}) async-start(), calls=%async_computation.7 | async-start | bytes 2621440 | tf_op jit(solution)/shard_map/reduce_scatter | solution.py:89
  355.7 1.3 copy-start.1
  355.7 30.3 %copy-start.8 = (f32[512,256]{1,0:T(8,128)S(1)}, f32[512,256]{1,0:T(8,128)}, u32[]{:S(2)}) copy-start(f32[512,256]{1,0:T(8,128)} %param.29) | copy-start | bytes 1572868
  355.7 30.2 %copy-start.15 = (f32[512,256]{1,0:T(8,128)S(1)}, f32[512,256]{1,0:T(8,128)}, u32[]{:S(2)}) copy-start(f32[512,256]{1,0:T(8,128)} %param.31) | copy-start | bytes 1572868
  355.8 30.2 %copy-start.20 = (f32[256]{0:T(256)S(1)}, f32[256]{0:T(256)}, u32[]{:S(2)}) copy-start(f32[256]{0:T(256)} %param.35) | copy-start | bytes 3076
  357.1 48.6 %all-gather.9.cloned.1.call-start = ((), (), s32[]{:S(2)}) async-start(), calls=%async_computation.8 | async-start | bytes 1310720 | tf_op jit(solution)/shard_map/all_gather | solution.py:86
  387.2 0.8 copy-start.4
  388.7 199.3 %reduce-scatter.9.cloned.1.call-start = ((), (), s32[]{:S(2)}) async-start(), calls=%async_computation.9 | async-start | bytes 4718592 | tf_op jit(solution)/shard_map/reduce_scatter | solution.py:100
  405.6 2.4 copy-start.3
  499.8 88.3 %copy-start.7 = (f32[512,256]{1,0:T(8,128)S(1)}, f32[512,256]{1,0:T(8,128)}, u32[]{:S(2)}) copy-start(f32[512,256]{1,0:T(8,128)} %copy-done.6) | copy-start | bytes 1572868
  499.8 88.3 %copy-start.10 = (f32[512,256]{1,0:T(8,128)S(1)}, f32[512,256]{1,0:T(8,128)}, u32[]{:S(2)}) copy-start(f32[512,256]{1,0:T(8,128)} %param.33) | copy-start | bytes 1572868
  499.8 88.3 %copy-start.12 = (f32[512,256]{1,0:T(8,128)S(1)}, f32[512,256]{1,0:T(8,128)}, u32[]{:S(2)}) copy-start(f32[512,256]{1,0:T(8,128)} %param.32) | copy-start | bytes 1572868
  499.8 88.3 %copy-start.14 = (f32[512,256]{1,0:T(8,128)S(1)}, f32[512,256]{1,0:T(8,128)}, u32[]{:S(2)}) copy-start(f32[512,256]{1,0:T(8,128)} %param.30) | copy-start | bytes 1572868
  499.8 139.7 %all-gather.11.cloned.1.call-start = ((), (), s32[]{:S(2)}) async-start(), calls=%async_computation.10 | async-start | bytes 2359296 | tf_op jit(solution)/shard_map/all_gather | solution.py:103
  590.2 173.5 %reduce-scatter.11.cloned.1.call-start = ((), (), s32[]{:S(2)}) async-start(), calls=%async_computation.11 | async-start | bytes 2621440 | tf_op jit(solution)/shard_map/reduce_scatter | solution.py:89
  733.4 1.3 copy-start
  733.4 30.3 %copy-start.5 = (f32[512,256]{1,0:T(8,128)S(1)}, f32[512,256]{1,0:T(8,128)}, u32[]{:S(2)}) copy-start(f32[512,256]{1,0:T(8,128)} %copy-done.4) | copy-start | bytes 1572868
  733.4 30.3 %copy-start.16 = (f32[512,256]{1,0:T(8,128)S(1)}, f32[512,256]{1,0:T(8,128)}, u32[]{:S(2)}) copy-start(f32[512,256]{1,0:T(8,128)} %param.31) | copy-start | bytes 1572868
Sparse Core Ops, SparseCore 0:
  10.1 19.4 all-gather.4
  123.9 86.7 reduce-scatter.4
  213.6 48.7 all-gather.6
  357.2 28.7 reduce-scatter.6
  388.9 16.7 all-gather.8
  499.9 88.0 reduce-scatter.8
  590.8 48.7 all-gather.10
  734.9 28.7 reduce-scatter.10
where the time goes:
time: 775 us; the launch traced here: 772 us
  waiting for transfers between devices  310 us (40%)
  other arithmetic  217 us (28%)
  matrix products  111 us (14%)
  local copies, waits for them, and re-layouts  77.6 us (10%)
  blocking collectives  40.9 us (5%)
  between operations  15 us (2%)
    reduce_scatter x2, waiting for transfers between devices, column_sums(): lax.psum_scatter(partial_value, 'row', scatter_dimension=0, tiled=True)  134 us
    scatter-add x12, other arithmetic, backward_block_step(): return running.at[col_block].add(products)  114 us
    all_gather x2, waiting for transfers between devices, spread(): return lax.all_gather(ahead, 'row', axis=0, tiled=True)  98.1 us
    scatter-add x12, other arithmetic, forward_block_step(): return running.at[row_block].add(products)  73.9 us
    dot_general x12, matrix products, forward_block_step(): jnp.einsum('sij,sjb->sib', tile_block, pieces, preferred_element_type=jnp...  59.4 us
    reduce_scatter x2, waiting for transfers between devices, row_sums(): lax.psum_scatter(forward_part(my_tiles, my_rows, my_cols, slot_count, seg...  57.8 us
    dot_general x12, matrix products, backward_block_step(): jnp.einsum('sij,sib->sjb', tile_block, pieces, preferred_element_type=jnp...  51.9 us
    gather x12, local copies, waits for them, and re-layouts, forward_block_step(): pieces = jnp.take(x_tiles, col_block, axis=0)  43.4 us
  transfers between devices with their start and end apart: 8, of which 8 were waited for; matrix products, arithmetic and copies ran while one was open for 2% of the time, Pallas kernels for 0%

commit v1 on v0

--- a/solution.py
+++ b/solution.py
@@ -70,6 +70,12 @@
     step_primal,
     step_dual,
 ):
+
+    def time_runs(inner_x, across, axis_tag):
+        for b in (across, axis_tag):
+            inner_x = lax.psum(inner_x, b)
+        return inner_x
+
     my_tiles = matrix_tiles[0, 0]
     my_rows = tile_rows[0, 0]
     my_cols = tile_cols[0, 0]
@@ -110,7 +116,7 @@
     dual_one = jnp.maximum(y_start + step_dual * (right_side - image_one), 0.0)
     dual_diff = dual_one - y_start
     move_dual = jnp.sum(dual_diff * dual_diff, axis=0)
-    move_primal, move_dual = lax.psum((move_primal, move_dual), ("row", "col"))
+    move_primal, move_dual = time_runs((move_primal, move_dual), "row", "col")
     weight = jnp.sqrt((move_dual / total_rows + eps) / (move_primal / total_cols + eps))
     grad_one = column_sums(dual_rows(dual_one))
     primal_two = jnp.clip(

time: 775 us -> 774 us (level)
  blocking collectives: 40.9 us -> 23.9 us
  waiting for transfers between devices: 310 us -> 326 us
    psum x1 -> x2, blocking collectives: 40.9 us -> 23.9 us  [time_runs(): inner_x = lax.psum(inner_x, b)]
    reduce_scatter x2, waiting for transfers between devices: 134 us -> 150 us  [column_sums(): lax.psum_scatter(partial_value, 'row', scatter_dimension=0, tiled=True)]
where the time goes in v1:
time: 774 us; the launch traced here: 771 us
  waiting for transfers between devices  326 us (42%)
  other arithmetic  217 us (28%)
  matrix products  112 us (14%)
  local copies, waits for them, and re-layouts  77.5 us (10%)
  blocking collectives  23.9 us (3%)
  between operations  14.9 us (2%)
    reduce_scatter x2, waiting for transfers between devices, column_sums(): lax.psum_scatter(partial_value, 'row', scatter_dimension=0, tiled=True)  150 us
    scatter-add x12, other arithmetic, backward_block_step(): return running.at[col_block].add(products)  114 us
    all_gather x2, waiting for transfers between devices, spread(): return lax.all_gather(ahead, 'row', axis=0, tiled=True)  98.1 us
    scatter-add x12, other arithmetic, forward_block_step(): return running.at[row_block].add(products)  73.9 us
    dot_general x12, matrix products, forward_block_step(): jnp.einsum('sij,sjb->sib', tile_block, pieces, preferred_element_type=jnp...  59.5 us
    reduce_scatter x2, waiting for transfers between devices, row_sums(): lax.psum_scatter(forward_part(my_tiles, my_rows, my_cols, slot_count, seg...  57.8 us
    dot_general x12, matrix products, backward_block_step(): jnp.einsum('sij,sib->sjb', tile_block, pieces, preferred_element_type=jnp...  52 us
    gather x12, local copies, waits for them, and re-layouts, forward_block_step(): pieces = jnp.take(x_tiles, col_block, axis=0)  43.3 us
  transfers between devices with their start and end apart: 8, of which 8 were waited for; matrix products, arithmetic and copies ran while one was open for 2% of the time, Pallas kernels for 0%

profile of v1, /device:TPU:0, one launch (start us, length us, event | category | flops | bytes accessed | tf_op | source)
XLA Modules:
  0.0 771.5 jit_solution(18286484827768753943)
XLA Ops:
  9.7 16.6 %copy.14 = bf16[96,256,256]{1,2,0:T(8,128)(2,1)} copy(bf16[96,256,256]{2,1,0:T(8,128)(2,1)} %bitcast.19) | data formatting | bytes 25165824
  32.0 91.7 %while.44 = (s32[]{:T(128)}, f32[16,256,256]{2,1,0:T(8,128)}, s32[]{:T(128)}, s32[96]{0:T(128)S(1)}, s32[]{:T(128)}, /*index=5*/bf16[96,256,256]{1,2,0:T(8,128)(...) while((s32[]{:T(128)}, f32[16,256,256]{2,1,0:T(8,128)}, ...), condition=%wide.region_2.4_spmd.clone, body=%wide.region_0.3_spmd.clone.sunk | while | flops 540017856 | bytes 25170616 | solution.py:56
  33.4 4.3 convolution_select_fusion.8
  37.8 9.5 %scatter_fusion = f32[16,256,256]{2,1,0:T(8,128)} fusion(f32[16,256,256]{2,1,0:T(8,128)} %get-tuple-element.617, s32[16]{0:T(128)S(1)} %compare_select_fusion.16, f32[16,256,256]{2,1,0:T(8,128)} %convolution_select_fusion.8), kind=kCustom, calls=%fused_computation.4.clone.clone.1 | custom fusion | flops 1048576 | bytes 12582976 | tf_op jit(solution)/shard_map/while/body/scatter-add | solution.py:52
  48.7 4.3 convolution_select_fusion.8
  53.2 9.5 %scatter_fusion = f32[16,256,256]{2,1,0:T(8,128)} fusion(f32[16,256,256]{2,1,0:T(8,128)} %get-tuple-element.617, s32[16]{0:T(128)S(1)} %compare_select_fusion.16, f32[16,256,256]{2,1,0:T(8,128)} %convolution_select_fusion.8), kind=kCustom, calls=%fused_computation.4.clone.clone.1 | custom fusion | flops 1048576 | bytes 12582976 | tf_op jit(solution)/shard_map/while/body/scatter-add | solution.py:52
  64.0 4.3 convolution_select_fusion.8
  68.5 9.5 %scatter_fusion = f32[16,256,256]{2,1,0:T(8,128)} fusion(f32[16,256,256]{2,1,0:T(8,128)} %get-tuple-element.617, s32[16]{0:T(128)S(1)} %compare_select_fusion.16, f32[16,256,256]{2,1,0:T(8,128)} %convolution_select_fusion.8), kind=kCustom, calls=%fused_computation.4.clone.clone.1 | custom fusion | flops 1048576 | bytes 12582976 | tf_op jit(solution)/shard_map/while/body/scatter-add | solution.py:52
  79.4 4.3 convolution_select_fusion.8
  83.8 9.5 %scatter_fusion = f32[16,256,256]{2,1,0:T(8,128)} fusion(f32[16,256,256]{2,1,0:T(8,128)} %get-tuple-element.617, s32[16]{0:T(128)S(1)} %compare_select_fusion.16, f32[16,256,256]{2,1,0:T(8,128)} %convolution_select_fusion.8), kind=kCustom, calls=%fused_computation.4.clone.clone.1 | custom fusion | flops 1048576 | bytes 12582976 | tf_op jit(solution)/shard_map/while/body/scatter-add | solution.py:52
  94.7 4.3 convolution_select_fusion.8
  99.1 9.3 %scatter_fusion = f32[16,256,256]{2,1,0:T(8,128)} fusion(f32[16,256,256]{2,1,0:T(8,128)} %get-tuple-element.617, s32[16]{0:T(128)S(1)} %compare_select_fusion.16, f32[16,256,256]{2,1,0:T(8,128)} %convolution_select_fusion.8), kind=kCustom, calls=%fused_computation.4.clone.clone.1 | custom fusion | flops 1048576 | bytes 12582976 | tf_op jit(solution)/shard_map/while/body/scatter-add | solution.py:52
  109.9 4.3 convolution_select_fusion.8
  114.3 9.4 %scatter_fusion = f32[16,256,256]{2,1,0:T(8,128)} fusion(f32[16,256,256]{2,1,0:T(8,128)} %get-tuple-element.617, s32[16]{0:T(128)S(1)} %compare_select_fusion.16, f32[16,256,256]{2,1,0:T(8,128)} %convolution_select_fusion.8), kind=kCustom, calls=%fused_computation.4.clone.clone.1 | custom fusion | flops 1048576 | bytes 12582976 | tf_op jit(solution)/shard_map/while/body/scatter-add | solution.py:52
  123.8 87.0 %reduce-scatter.5.cloned.1.call-done = f32[512,256]{1,0:T(8,128)} async-done(((f32[4096,256]{1,0:T(8,128)}), f32[512,256]{1,0:T(8,128)}) %reduce-scatter.5.cloned.1.call-update) | async-done | bytes 524304 | tf_op jit(solution)/shard_map/reduce_scatter | solution.py:106
  213.6 48.8 %all-gather.7.cloned.1.call-done = bf16[4096,256]{1,0:T(8,128)(2,1)} async-done(((bf16[512,256]{1,0:T(8,128)(2,1)}), bf16[4096,256]{1,0:T(8,128)(2,1)}) %all-gather.7.cloned.1.call-update) | async-done | bytes 2097168 | tf_op jit(solution)/shard_map/all_gather | solution.py:109
  262.6 93.3 %while.45 = (s32[]{:T(128)}, f32[8,256,256]{2,1,0:T(8,128)S(1)}, s32[]{:T(128)}, s32[96]{0:T(128)S(1)}, s32[]{:T(128)}, /*index=5*/bf16[96,256,256]{2,1,0:T(8,12...) while((s32[]{:T(128)}, f32[8,256,256]{2,1,0:T(8,128)S(1)}, ...), condition=%wide.region_6.9_spmd.clone, body=%wide.region_4.8_spmd.clone.sunk | while | flops 540017856 | bytes 25170616 | solution.py:32
  267.0 5.0 convolution_select_fusion.9
  272.0 6.1 scatter_fusion.1
  282.5 5.0 convolution_select_fusion.9
  287.5 6.2 scatter_fusion.1
  298.1 5.0 convolution_select_fusion.9
  303.1 6.1 scatter_fusion.1
  313.6 5.0 convolution_select_fusion.9
  318.6 6.2 scatter_fusion.1
  329.2 5.0 convolution_select_fusion.9
  334.2 6.1 scatter_fusion.1
  344.7 5.0 convolution_select_fusion.9
  349.7 6.2 scatter_fusion.1
  357.3 28.9 %reduce-scatter.7.cloned.1.call-done = f32[512,256]{1,0:T(8,128)} async-done(((f32[2048,256]{1,0:T(8,128)}), f32[512,256]{1,0:T(8,128)}) %reduce-scatter.7.cloned.1.call-update) | async-done | bytes 524304 | tf_op jit(solution)/shard_map/reduce_scatter | solution.py:95
  389.0 16.8 %all-gather.9.cloned.1.call-done = bf16[2048,256]{1,0:T(8,128)(2,1)} async-done(((bf16[512,256]{1,0:T(8,128)(2,1)}), bf16[2048,256]{1,0:T(8,128)(2,1)}) %all-gather.9.cloned.1.call-update) | async-done | bytes 1048592 | tf_op jit(solution)/shard_map/all_gather | solution.py:92
  408.2 91.9 %while.46 = (s32[]{:T(128)}, f32[16,256,256]{2,1,0:T(8,128)}, s32[]{:T(128)}, s32[96]{0:T(128)S(1)}, s32[]{:T(128)}, /*index=5*/bf16[96,256,256]{1,2,0:T(8,128)(...) while((s32[]{:T(128)}, f32[16,256,256]{2,1,0:T(8,128)}, ...), condition=%wide.region_16.19_spmd.clone, body=%wide.region_14.18_spmd.clone.sunk | while | flops 540017856 | bytes 25170616 | solution.py:56
  409.6 4.3 convolution_select_fusion.10
  414.0 9.5 %scatter_fusion.2 = f32[16,256,256]{2,1,0:T(8,128)} fusion(f32[16,256,256]{2,1,0:T(8,128)} %get-tuple-element.689, s32[16]{0:T(128)S(1)} %compare_select_fusion.18, f32[16,256,256]{2,1,0:T(8,128)} %convolution_select_fusion.10), kind=kCustom, calls=%fused_computation.6.clone.clone.1 | custom fusion | flops 1048576 | bytes 12582976 | tf_op jit(solution)/shard_map/while/body/scatter-add | solution.py:52
  424.9 4.3 convolution_select_fusion.10
  429.3 9.6 %scatter_fusion.2 = f32[16,256,256]{2,1,0:T(8,128)} fusion(f32[16,256,256]{2,1,0:T(8,128)} %get-tuple-element.689, s32[16]{0:T(128)S(1)} %compare_select_fusion.18, f32[16,256,256]{2,1,0:T(8,128)} %convolution_select_fusion.10), kind=kCustom, calls=%fused_computation.6.clone.clone.1 | custom fusion | flops 1048576 | bytes 12582976 | tf_op jit(solution)/shard_map/while/body/scatter-add | solution.py:52
  440.3 4.3 convolution_select_fusion.10
  444.8 9.5 %scatter_fusion.2 = f32[16,256,256]{2,1,0:T(8,128)} fusion(f32[16,256,256]{2,1,0:T(8,128)} %get-tuple-element.689, s32[16]{0:T(128)S(1)} %compare_select_fusion.18, f32[16,256,256]{2,1,0:T(8,128)} %convolution_select_fusion.10), kind=kCustom, calls=%fused_computation.6.clone.clone.1 | custom fusion | flops 1048576 | bytes 12582976 | tf_op jit(solution)/shard_map/while/body/scatter-add | solution.py:52
  455.7 4.3 convolution_select_fusion.10
  460.1 9.4 %scatter_fusion.2 = f32[16,256,256]{2,1,0:T(8,128)} fusion(f32[16,256,256]{2,1,0:T(8,128)} %get-tuple-element.689, s32[16]{0:T(128)S(1)} %compare_select_fusion.18, f32[16,256,256]{2,1,0:T(8,128)} %convolution_select_fusion.10), kind=kCustom, calls=%fused_computation.6.clone.clone.1 | custom fusion | flops 1048576 | bytes 12582976 | tf_op jit(solution)/shard_map/while/body/scatter-add | solution.py:52
  471.0 4.3 convolution_select_fusion.10
  475.4 9.4 %scatter_fusion.2 = f32[16,256,256]{2,1,0:T(8,128)} fusion(f32[16,256,256]{2,1,0:T(8,128)} %get-tuple-element.689, s32[16]{0:T(128)S(1)} %compare_select_fusion.18, f32[16,256,256]{2,1,0:T(8,128)} %convolution_select_fusion.10), kind=kCustom, calls=%fused_computation.6.clone.clone.1 | custom fusion | flops 1048576 | bytes 12582976 | tf_op jit(solution)/shard_map/while/body/scatter-add | solution.py:52
  486.2 4.3 convolution_select_fusion.10
  490.6 9.5 %scatter_fusion.2 = f32[16,256,256]{2,1,0:T(8,128)} fusion(f32[16,256,256]{2,1,0:T(8,128)} %get-tuple-element.689, s32[16]{0:T(128)S(1)} %compare_select_fusion.18, f32[16,256,256]{2,1,0:T(8,128)} %convolution_select_fusion.10), kind=kCustom, calls=%fused_computation.6.clone.clone.1 | custom fusion | flops 1048576 | bytes 12582976 | tf_op jit(solution)/shard_map/while/body/scatter-add | solution.py:52
  500.2 17.8 %all-reduce = (f32[256]{0:T(256)S(1)}, f32[256]{0:T(256)S(1)}) all-reduce(f32[256]{0:T(256)S(1)} %get-tuple-element.374, f32[256]{0:T(256)S(1)} %get-tuple-element.372), channel_id=1, replica_groups=mesh['row'=8,'col'=4] {'row'}, use_global_device_ids=true, to_apply=%region_12.15 | all-reduce | flops 512 | bytes 4096 | tf_op jit(solution)/shard_map/psum | solution.py:76
  518.0 6.0 all-reduce.1
  524.1 63.0 %reduce-scatter.9.cloned.1.call-done = f32[512,256]{1,0:T(8,128)} async-done(((f32[4096,256]{1,0:T(8,128)}), f32[512,256]{1,0:T(8,128)}) %reduce-scatter.9.cloned.1.call-update) | async-done | bytes 524304 | tf_op jit(solution)/shard_map/reduce_scatter | solution.py:106
  589.3 49.3 %all-gather.11.cloned.1.call-done = bf16[4096,256]{1,0:T(8,128)(2,1)} async-done(((bf16[512,256]{1,0:T(8,128)(2,1)}), bf16[4096,256]{1,0:T(8,128)(2,1)}) %all-gather.11.cloned.1.call-update) | async-done | bytes 2097168 | tf_op jit(solution)/shard_map/all_gather | solution.py:109
  638.7 93.6 %while.47 = (s32[]{:T(128)}, f32[8,256,256]{2,1,0:T(8,128)S(1)}, s32[]{:T(128)}, s32[96]{0:T(128)S(1)}, s32[]{:T(128)}, /*index=5*/bf16[96,256,256]{2,1,0:T(8,12...) while((s32[]{:T(128)}, f32[8,256,256]{2,1,0:T(8,128)S(1)}, ...), condition=%wide.region_20.23_spmd.clone, body=%wide.region_18.22_spmd.clone.sunk | while | flops 540017856 | bytes 25170616 | solution.py:32
  639.5 3.6 gather_fusion.3
  643.1 5.0 convolution_select_fusion.11
  648.2 6.1 scatter_fusion.3
  655.1 3.6 gather_fusion.3
  658.7 5.0 convolution_select_fusion.11
  663.8 6.2 scatter_fusion.3
  674.4 5.0 convolution_select_fusion.11
  679.4 6.1 scatter_fusion.3
  690.0 5.0 convolution_select_fusion.11
  695.0 6.2 scatter_fusion.3
  705.6 5.0 convolution_select_fusion.11
  710.6 6.1 scatter_fusion.3
  721.2 5.0 convolution_select_fusion.11
  726.2 6.2 scatter_fusion.3
  733.7 28.9 %reduce-scatter.11.cloned.1.call-done = f32[512,256]{1,0:T(8,128)} async-done(((f32[2048,256]{1,0:T(8,128)}), f32[512,256]{1,0:T(8,128)}) %reduce-scatter.11.cloned.1.call-update) | async-done | bytes 524304 | tf_op jit(solution)/shard_map/reduce_scatter | solution.py:95
  (168 shorter events, 86.3 us)
Async XLA Ops:
  7.2 22.4 %all-gather.5.cloned.1.call-start = ((), (), s32[]{:S(2)}) async-start(), calls=%async_computation.4 | async-start | bytes 1310720 | tf_op jit(solution)/shard_map/all_gather | solution.py:92
  9.0 201.8 %reduce-scatter.5.cloned.1.call-start = ((), (), s32[]{:S(2)}) async-start(), calls=%async_computation.5 | async-start | bytes 4718592 | tf_op jit(solution)/shard_map/reduce_scatter | solution.py:106
  29.6 2.4 copy-start.2
  29.6 2.4 copy-start.18
  29.6 2.4 copy-start.19
  123.7 87.1 %copy-start.9 = (f32[512,256]{1,0:T(8,128)S(1)}, f32[512,256]{1,0:T(8,128)}, u32[]{:S(2)}) copy-start(f32[512,256]{1,0:T(8,128)} %param.33) | copy-start | bytes 1572868
  123.7 87.1 %copy-start.11 = (f32[512,256]{1,0:T(8,128)S(1)}, f32[512,256]{1,0:T(8,128)}, u32[]{:S(2)}) copy-start(f32[512,256]{1,0:T(8,128)} %param.32) | copy-start | bytes 1572868
  123.7 87.1 %copy-start.13 = (f32[512,256]{1,0:T(8,128)S(1)}, f32[512,256]{1,0:T(8,128)}, u32[]{:S(2)}) copy-start(f32[512,256]{1,0:T(8,128)} %param.30) | copy-start | bytes 1572868
  123.7 87.1 %copy-start.17 = (f32[512,256]{1,0:T(8,128)S(1)}, f32[512,256]{1,0:T(8,128)}, u32[]{:S(2)}) copy-start(f32[512,256]{1,0:T(8,128)} %param.28) | copy-start | bytes 1572868
  123.7 87.1 %copy-start.21 = (f32[256]{0:T(256)S(1)}, f32[256]{0:T(256)}, u32[]{:S(2)}) copy-start(f32[256]{0:T(256)} %param.34) | copy-start | bytes 3076
  123.7 138.7 %all-gather.7.cloned.1.call-start = ((), (), s32[]{:S(2)}) async-start(), calls=%async_computation.6 | async-start | bytes 2359296 | tf_op jit(solution)/shard_map/all_gather | solution.py:109
  212.0 0.8 copy-start.6
  213.6 172.6 %reduce-scatter.7.cloned.1.call-start = ((), (), s32[]{:S(2)}) async-start(), calls=%async_computation.7 | async-start | bytes 2621440 | tf_op jit(solution)/shard_map/reduce_scatter | solution.py:95
  355.9 1.3 copy-start.1
  355.9 30.3 %copy-start.8 = (f32[512,256]{1,0:T(8,128)S(1)}, f32[512,256]{1,0:T(8,128)}, u32[]{:S(2)}) copy-start(f32[512,256]{1,0:T(8,128)} %param.29) | copy-start | bytes 1572868
  355.9 30.3 %copy-start.15 = (f32[512,256]{1,0:T(8,128)S(1)}, f32[512,256]{1,0:T(8,128)}, u32[]{:S(2)}) copy-start(f32[512,256]{1,0:T(8,128)} %param.31) | copy-start | bytes 1572868
  355.9 30.2 %copy-start.20 = (f32[256]{0:T(256)S(1)}, f32[256]{0:T(256)}, u32[]{:S(2)}) copy-start(f32[256]{0:T(256)} %param.35) | copy-start | bytes 3076
  357.2 48.6 %all-gather.9.cloned.1.call-start = ((), (), s32[]{:S(2)}) async-start(), calls=%async_computation.8 | async-start | bytes 1310720 | tf_op jit(solution)/shard_map/all_gather | solution.py:92
  387.4 0.8 copy-start.4
  388.9 198.2 %reduce-scatter.9.cloned.1.call-start = ((), (), s32[]{:S(2)}) async-start(), calls=%async_computation.9 | async-start | bytes 4718592 | tf_op jit(solution)/shard_map/reduce_scatter | solution.py:106
  405.8 2.4 copy-start.3
  500.1 87.0 %copy-start.7 = (f32[512,256]{1,0:T(8,128)S(1)}, f32[512,256]{1,0:T(8,128)}, u32[]{:S(2)}) copy-start(f32[512,256]{1,0:T(8,128)} %copy-done.6) | copy-start | bytes 1572868
  500.1 87.0 %copy-start.10 = (f32[512,256]{1,0:T(8,128)S(1)}, f32[512,256]{1,0:T(8,128)}, u32[]{:S(2)}) copy-start(f32[512,256]{1,0:T(8,128)} %param.33) | copy-start | bytes 1572868
  500.1 87.0 %copy-start.12 = (f32[512,256]{1,0:T(8,128)S(1)}, f32[512,256]{1,0:T(8,128)}, u32[]{:S(2)}) copy-start(f32[512,256]{1,0:T(8,128)} %param.32) | copy-start | bytes 1572868
  500.1 87.0 %copy-start.14 = (f32[512,256]{1,0:T(8,128)S(1)}, f32[512,256]{1,0:T(8,128)}, u32[]{:S(2)}) copy-start(f32[512,256]{1,0:T(8,128)} %param.30) | copy-start | bytes 1572868
  500.1 138.4 %all-gather.11.cloned.1.call-start = ((), (), s32[]{:S(2)}) async-start(), calls=%async_computation.10 | async-start | bytes 2359296 | tf_op jit(solution)/shard_map/all_gather | solution.py:109
  589.2 173.5 %reduce-scatter.11.cloned.1.call-start = ((), (), s32[]{:S(2)}) async-start(), calls=%async_computation.11 | async-start | bytes 2621440 | tf_op jit(solution)/shard_map/reduce_scatter | solution.py:95
  732.4 1.3 copy-start
  732.4 30.3 %copy-start.5 = (f32[512,256]{1,0:T(8,128)S(1)}, f32[512,256]{1,0:T(8,128)}, u32[]{:S(2)}) copy-start(f32[512,256]{1,0:T(8,128)} %copy-done.4) | copy-start | bytes 1572868
  732.4 30.3 %copy-start.16 = (f32[512,256]{1,0:T(8,128)S(1)}, f32[512,256]{1,0:T(8,128)}, u32[]{:S(2)}) copy-start(f32[512,256]{1,0:T(8,128)} %param.31) | copy-start | bytes 1572868
Sparse Core Ops, SparseCore 0:
  10.1 19.4 all-gather.4
  123.9 86.8 reduce-scatter.4
  213.7 48.7 all-gather.6
  357.4 28.7 reduce-scatter.6
  389.0 16.7 all-gather.8
  500.3 86.7 reduce-scatter.8
  589.8 48.7 all-gather.10
  733.9 28.7 reduce-scatter.10
